TPU v7x, 32 devices: a whole 2x2x4 slice. The times are simulated.
32 devices in a mesh: island: 16 (over z, y, x), tensor: 2 (over core).
Axes of the slice: x: 2, y: 2, z: 4, core: 2. Of those that a mesh axis runs over, the one named last changes fastest.
Arguments:
- pseudo_grad: float32 [16, 32, 53248], P('island', None, 'tensor'), may hold values from -8000 to 8000
- outer_params: float32 [32, 53248], P('island', 'tensor'), may hold values from -4 to 4
- momentum: float32 [32, 53248], P('island', 'tensor'), may hold values from -6 to 6
- save_pages: int32 [16], replicated, may hold values from 1 to 832, 6656 in all
- writer: int32 [16], replicated, may hold values from 0 to 15, each once
Outputs:
- new_master: float32 [32, 53248], P('island', 'tensor')
- new_momentum: float32 [32, 53248], P('island', 'tensor')
- checkpoint: bfloat16 [16, 832, 256], P('island', None, 'tensor')
Inputs may be any that keep to these rules, and one draw needn't show every extreme that they name: save_pages sums to 6656; the longest range has exactly 832 pages. writer names every island once.
All inputs are finite; a program needn't handle non-finite values.
Results may differ from a plain program's by a relative error of at most 0.0007.
Values may be sent and summed in bfloat16 or wider, within the bound.
A program may use at most 64 MiB of HBM per device.

v0:
```python
import jax
import jax.numpy as jnp
from jax import lax
from jax.sharding import PartitionSpec as P

epsilon = 1e-06
decay_rate = 0.9
outer_rate = 0.7


def body(pseudo_grad, outer_params, momentum, save_pages, writer):
    own_rows = outer_params.shape[0]
    col_width = outer_params.shape[1]
    islands = lax.axis_size("island")
    my_index = lax.axis_index("island")
    own_grad = pseudo_grad[0]
    entries = own_grad.shape[0] * col_width * lax.axis_size("tensor")
    summed = lax.psum(own_grad, "island")
    full_grad = summed / islands
    square_sum = lax.psum(jnp.sum(full_grad * full_grad), "tensor")
    outer_grad = lax.dynamic_slice_in_dim(full_grad, my_index * own_rows, own_rows, 0)
    normed = outer_grad / jnp.sqrt(square_sum / entries + epsilon)
    new_momentum = decay_rate * momentum + normed
    new_master = outer_params - outer_rate * (normed + decay_rate * new_momentum)
    cast_rows = new_master.astype(jnp.bfloat16)
    pages_own = own_rows * col_width // 128
    capacity = 2 * pages_own
    starts = jnp.cumsum(save_pages) - save_pages
    targets = jnp.arange(islands, dtype=jnp.int32)
    owner_table = writer[None, :] == targets[:, None]
    range_start = jnp.sum(jnp.where(owner_table, starts[None, :], 0), axis=1)
    range_length = jnp.sum(jnp.where(owner_table, save_pages[None, :], 0), axis=1)
    is_mine = targets == my_index
    own_start = jnp.sum(jnp.where(is_mine, range_start, 0))
    own_length = jnp.sum(jnp.where(is_mine, range_length, 0))
    slot_ids = jnp.arange(capacity, dtype=jnp.int32)
    own_pages = cast_rows.reshape(pages_own, 128)
    spread_slots = -(-pages_own // islands)
    deliver_slots = -(-capacity // islands)
    spread_ids = jnp.arange(spread_slots, dtype=jnp.int32)
    offset = jnp.mod(targets - my_index * pages_own, islands)
    local_index = offset[:, None] + islands * spread_ids[None, :]
    live_slot = (local_index < pages_own).reshape(-1, 1)
    outgoing = jnp.take(own_pages, jnp.clip(local_index, 0, pages_own - 1).reshape(-1), axis=0)
    outgoing = jnp.where(live_slot, outgoing, jnp.zeros_like(outgoing))
    spread = lax.all_to_all(outgoing, "island", split_axis=0, concat_axis=0, tiled=True)
    deliver_ids = jnp.arange(deliver_slots, dtype=jnp.int32)
    first_page = range_start + jnp.mod(my_index - range_start, islands)
    global_page = first_page[:, None] + islands * deliver_ids[None, :]
    live_out = (global_page < (range_start + range_length)[:, None]).reshape(-1, 1)
    held_index = (
        global_page // pages_own * spread_slots + jnp.mod(global_page, pages_own) // islands
    )
    held_index = jnp.clip(held_index, 0, islands * spread_slots - 1).reshape(-1)
    forward = jnp.take(spread, held_index, axis=0)
    forward = jnp.where(live_out, forward, jnp.zeros_like(forward))
    delivered = lax.all_to_all(forward, "island", split_axis=0, concat_axis=0, tiled=True)
    source = jnp.mod(own_start + slot_ids, islands) * deliver_slots + slot_ids // islands
    source = jnp.clip(source, 0, islands * deliver_slots - 1)
    packed = jnp.take(delivered, source, axis=0)
    packed = jnp.where((slot_ids < own_length)[:, None], packed, jnp.zeros_like(packed))
    return (new_master, new_momentum, packed[None])


def solution(mesh):
    in_specs = (P("island", None, "tensor"), P("island", "tensor"), P("island", "tensor"), P(), P())
    out_specs = (P("island", "tensor"), P("island", "tensor"), P("island", None, "tensor"))
    return jax.shard_map(body, mesh=mesh, in_specs=in_specs, out_specs=out_specs, check_vma=False)
```

profile of v0, /device:TPU:0, one launch (start us, length us, event | category | flops | bytes accessed | tf_op | source)
XLA Modules:
  0.0 218.6 jit_solution(9376555139836277744)
XLA Ops:
  7.2 0.0 copy-start
  7.2 0.0 copy-start.1
  7.2 0.0 all-reduce.2.cloned.1.call-start
  7.2 0.7 all-reduce.2.cloned.1.call-update
  8.0 0.1 add_clamp_fusion
  8.0 0.1 min.40
  8.1 0.0 copy-done
  8.1 0.1 copy.10
  8.3 0.1 reduce
  8.4 0.0 copy-done.1
  8.4 0.1 select_reduce_fusion.1
  8.5 0.7 fusion.32
  9.2 0.1 add_divide_fusion
  9.3 0.1 rem.175
  9.4 0.1 div.75
  9.5 0.1 add_compare_fusion
  9.6 0.1 ne.202
  9.7 0.1 add_compare_fusion.1
  9.8 159.0 %all-reduce.2.cloned.1.call-done = f32[32,26624]{1,0:T(8,128)} async-done(((f32[32,26624]{1,0:T(8,128)}), f32[32,26624]{1,0:T(8,128)}) %all-reduce.2.cloned.1.call-update) | async-done | bytes 3407888 | tf_op jit(solution)/shard_map/psum | solution.py:18
  168.8 3.5 %broadcast_multiply_fusion = (f32[32,26624]{1,0:T(8,128)S(1)}, f32[]{:T(128)}) fusion(f32[32,26624]{1,0:T(8,128)} %all-reduce.2.cloned.1.call-done), kind=kLoop, calls=%fused_computation.4 | loop fusion | flops 2555903 | bytes 6815748 | tf_op jit(solution)/shard_map/div | solution.py:19
  172.2 3.1 %psum.15 = f32[]{:T(128)} all-reduce(f32[]{:T(128)} %get-tuple-element.9), channel_id=1, replica_groups=mesh['island'=16,'tensor'=2] {'tensor'}, use_global_device_ids=true, to_apply=%region_2.0 | all-reduce | flops 1 | bytes 8 | tf_op jit(solution)/shard_map/psum | solution.py:20
  176.0 2.1 fusion.36
  178.1 0.1 reshape.458
  178.2 1.5 gather_fusion
  179.7 0.9 select_select_fusion.1
  180.6 4.7 %all-to-all-start = ((bf16[16,26,128]{2,1,0:T(8,128)(2,1)}), bf16[16,26,128]{2,1,0:T(8,128)(2,1)S(1)}, u32[]{:S(2)}, u32[]{:S(2)}) async-start(bf16[16,26,128]{2,1,0:T(8,128)(2,1)} %select_select_fusion.1), calls=%async_computation | async-start | bytes 262144 | tf_op jit(solution)/shard_map/all_to_all | solution.py:46
  185.3 0.1 fusion.25
  185.4 7.7 %all-to-all-done = bf16[16,26,128]{2,1,0:T(8,128)(2,1)S(1)} async-done(((bf16[16,26,128]{2,1,0:T(8,128)(2,1)}), bf16[16,26,128]{2,1,0:T(8,128)(2,1)S(1)}, u32[]{:S(2)}, u32[]{:S(2)}) %all-to-all-start) | async-done | bytes 106528 | tf_op jit(solution)/shard_map/all_to_all | solution.py:46
  193.1 2.4 %gather_fusion.1 = bf16[832,128]{1,0:T(8,128)(2,1)S(1)} fusion(bf16[416,128]{1,0:T(8,128)(2,1)S(1)} %all_to_all.13, s32[1024]{0:T(1024)S(1)} %pad_clamp_fusion.1), kind=kCustom, calls=%fused_computation.1 | custom fusion | bytes 429312 | tf_op jit(solution)/shard_map/jit(_take)/gather | solution.py:55
  195.5 1.0 select_select_fusion
  196.5 3.5 %all-to-all-start.1 = ((bf16[16,52,128]{2,1,0:T(8,128)(2,1)}), bf16[16,52,128]{2,1,0:T(8,128)(2,1)S(1)}, u32[]{:S(2)}, u32[]{:S(2)}) async-start(bf16[16,52,128]{2,1,0:T(8,128)(2,1)} %select_select_fusion), calls=%async_computation.1 | async-start | bytes 458752 | tf_op jit(solution)/shard_map/all_to_all | solution.py:57
  200.1 0.7 fusion.26
  200.8 1.3 iota_compare_fusion.1
  202.1 6.3 %all-to-all-done.1 = bf16[16,52,128]{2,1,0:T(8,128)(2,1)S(1)} async-done(((bf16[16,52,128]{2,1,0:T(8,128)(2,1)}), bf16[16,52,128]{2,1,0:T(8,128)(2,1)S(1)}, u32[]{:S(2)}, u32[]{:S(2)}) %all-to-all-start.1) | async-done | bytes 213024 | tf_op jit(solution)/shard_map/all_to_all | solution.py:57
  208.4 2.4 %gather_fusion.2 = bf16[832,128]{1,0:T(8,128)(2,1)S(1)} fusion(bf16[832,128]{1,0:T(8,128)(2,1)S(1)} %all_to_all.15, s32[1024]{0:T(1024)S(1)} %pad_clamp_fusion), kind=kCustom, calls=%fused_computation.2 | custom fusion | bytes 429312 | tf_op jit(solution)/shard_map/jit(_take)/gather | solution.py:60
  210.8 1.0 fusion
  (13 shorter events, 0.2 us)
Async XLA Ops:
  7.2 1.0 copy-start
  7.2 1.2 copy-start.1
  7.2 161.6 %all-reduce.2.cloned.1.call-start = ((), (), s32[]{:S(2)}) async-start(), calls=%async_computation.2 | async-start | bytes 6815744 | tf_op jit(solution)/shard_map/psum | solution.py:18
  180.6 12.5 %all-to-all-start = ((bf16[16,26,128]{2,1,0:T(8,128)(2,1)}), bf16[16,26,128]{2,1,0:T(8,128)(2,1)S(1)}, u32[]{:S(2)}, u32[]{:S(2)}) async-start(bf16[16,26,128]{2,1,0:T(8,128)(2,1)} %select_select_fusion.1), calls=%async_computation | async-start | bytes 262144 | tf_op jit(solution)/shard_map/all_to_all | solution.py:46
  196.5 11.8 %all-to-all-start.1 = ((bf16[16,52,128]{2,1,0:T(8,128)(2,1)}), bf16[16,52,128]{2,1,0:T(8,128)(2,1)S(1)}, u32[]{:S(2)}, u32[]{:S(2)}) async-start(bf16[16,52,128]{2,1,0:T(8,128)(2,1)} %select_select_fusion), calls=%async_computation.1 | async-start | bytes 458752 | tf_op jit(solution)/shard_map/all_to_all | solution.py:57
Sparse Core Ops, SparseCore 0:
  13.7 155.0 all-reduce.1
where the time goes:
time: 219 us
  waiting for transfers between devices  174 us (79%)
  between operations  14.9 us (7%)
  other arithmetic  11.8 us (5%)
  starting transfers between devices  8.25 us (4%)
  local copies, waits for them, and re-layouts  6.87 us (3%)
  blocking collectives  3.08 us (1%)
    psum x1, waiting for transfers between devices, body(): summed = lax.psum(own_grad, 'island')  159 us
    all_to_all x1, waiting for transfers between devices, body(): lax.all_to_all(outgoing, 'island', split_axis=0, concat_axis=0, tiled=True)  7.72 us
    all_to_all x1, waiting for transfers between devices, body(): lax.all_to_all(forward, 'island', split_axis=0, concat_axis=0, tiled=True)  6.3 us
    all_to_all x1, starting transfers between devices, body(): lax.all_to_all(outgoing, 'island', split_axis=0, concat_axis=0, tiled=True)  4.69 us
  transfers between devices with their start and end apart: 3, of which 3 were waited for; matrix products, arithmetic and copies ran while one was open for 2% of the time, Pallas kernels for 0%

commit v1 on v0

--- a/solution.py
+++ b/solution.py
@@ -15,7 +15,9 @@
     my_index = lax.axis_index("island")
     own_grad = pseudo_grad[0]
     entries = own_grad.shape[0] * col_width * lax.axis_size("tensor")
-    summed = lax.psum(own_grad, "island")
+    summed = own_grad
+    for hop in (1, 2, 4, 8):
+        summed = summed + lax.ppermute(summed, "island", [(dev, dev ^ hop) for dev in range(16)])
     full_grad = summed / islands
     square_sum = lax.psum(jnp.sum(full_grad * full_grad), "tensor")
     outer_grad = lax.dynamic_slice_in_dim(full_grad, my_index * own_rows, own_rows, 0)

time: 219 us -> 424 us (1.94)
  waiting for transfers between devices: 174 us -> 377 us
  between operations: 14.9 us -> 1.51 us
  starting transfers between devices: 8.25 us -> 18.5 us
  other arithmetic: 11.8 us -> 16.7 us
    ppermute x0 -> x4, waiting for transfers between devices: none -> 363 us  [body(): lax.ppermute(summed, 'island', [(dev, dev ^ hop) for dev in range(16)])]
    psum x1 -> x0, waiting for transfers between devices: 159 us -> none  [body(): summed = lax.psum(own_grad, 'island')]
    ppermute x0 -> x4, starting transfers between devices: none -> 8.82 us  [body(): lax.ppermute(summed, 'island', [(dev, dev ^ hop) for dev in range(16)])]
    reduce_sum x0 -> x1, other arithmetic: none -> 5.16 us  [body(): square_sum = lax.psum(jnp.sum(full_grad * full_grad), 'tensor')]
  transfers between devices with their start and end apart: 3 -> 6, of which waited for: 3 -> 6; matrix products, arithmetic and copies ran while one was open for 2% -> 1% of each run, Pallas kernels for 0% -> 0%
where the time goes in v1:
time: 424 us; the launch traced here: 423 us
  waiting for transfers between devices  377 us (89%)
  starting transfers between devices  18.5 us (4%)
  other arithmetic  16.7 us (4%)
  local copies, waits for them, and re-layouts  6.87 us (2%)
    ppermute x4, waiting for transfers between devices, body(): lax.ppermute(summed, 'island', [(dev, dev ^ hop) for dev in range(16)])  363 us
    ppermute x4, starting transfers between devices, body(): lax.ppermute(summed, 'island', [(dev, dev ^ hop) for dev in range(16)])  8.82 us
  transfers between devices with their start and end apart: 6, of which 6 were waited for; matrix products, arithmetic and copies ran while one was open for 1% of the time, Pallas kernels for 0%

profile of v1, /device:TPU:0, one launch (start us, length us, event | category | flops | bytes accessed | tf_op | source)
XLA Modules:
  0.0 423.4 jit_solution(7514321474841438113)
XLA Ops:
  0.6 3.0 collective-permute-start
  3.7 73.9 %collective-permute-done = f32[32,26624]{1,0:T(8,128)S(1)} collective-permute-done((f32[32,26624]{1,0:T(8,128)}, f32[32,26624]{1,0:T(8,128)S(1)}, u32[]{:S(2)}, u32[]{:S(2)}) %collective-permute-start) | collective-permute-done | bytes 3407904 | tf_op jit(solution)/shard_map/ppermute | solution.py:20
  77.6 2.4 bitcast_add_fusion
  80.0 1.8 collective-permute-start.1
  81.9 73.1 %collective-permute-done.1 = f32[32,26624]{1,0:T(8,128)S(1)} collective-permute-done((f32[32,26624]{1,0:T(8,128)S(1)}, f32[32,26624]{1,0:T(8,128)S(1)}, u32[]{:S(2)}, u32[]{:S(2)}) %collective-permute-start.1) | collective-permute-done | bytes 3407904 | tf_op jit(solution)/shard_map/ppermute | solution.py:20
  155.0 0.3 add.291
  155.3 0.0 copy-start
  155.3 0.0 copy-start.1
  155.3 1.6 collective-permute-start.2
  156.9 72.5 %collective-permute-done.2 = f32[32,26624]{1,0:T(8,128)S(1)} collective-permute-done((f32[32,26624]{1,0:T(8,128)S(1)}, f32[32,26624]{1,0:T(8,128)S(1)}, u32[]{:S(2)}, u32[]{:S(2)}) %collective-permute-start.2) | collective-permute-done | bytes 3407904 | tf_op jit(solution)/shard_map/ppermute | solution.py:20
  229.4 0.3 add.292
  229.8 2.3 collective-permute-start.3
  232.1 0.1 add_clamp_fusion
  232.2 0.1 min.40
  232.3 0.0 copy-done
  232.3 0.1 copy.10
  232.4 0.1 reduce
  232.6 0.0 copy-done.1
  232.6 0.1 select_reduce_fusion.1
  232.7 0.7 fusion.32
  233.4 0.1 add_compare_fusion
  233.5 0.1 ne.202
  233.6 0.1 add_divide_fusion
  233.7 0.1 div.75
  233.8 0.1 rem.175
  233.9 0.1 add_compare_fusion.1
  234.0 143.1 %collective-permute-done.3 = f32[32,26624]{1,0:T(8,128)} collective-permute-done((f32[32,26624]{1,0:T(8,128)S(1)}, f32[32,26624]{1,0:T(8,128)}, u32[]{:S(2)}, u32[]{:S(2)}) %collective-permute-start.3) | collective-permute-done | bytes 3407904 | tf_op jit(solution)/shard_map/ppermute | solution.py:20
  377.0 5.2 %multiply_reduce_fusion = (f32[]{:T(128)}, f32[32,26624]{1,0:T(8,128)}) fusion(f32[32,26624]{1,0:T(8,128)S(1)} %add.292, f32[32,26624]{1,0:T(8,128)} %collective-permute-done.3), kind=kLoop, calls=%fused_computation.3 | loop fusion | flops 3407871 | bytes 10223620 | tf_op jit(solution)/shard_map/reduce_sum | solution.py:22
  382.2 3.1 psum.7
  386.0 2.3 fusion.36
  388.3 0.1 reshape.458
  388.4 1.5 gather_fusion
  389.9 0.9 select_select_fusion.1
  390.8 6.2 %all-to-all-start = ((bf16[16,26,128]{2,1,0:T(8,128)(2,1)}), bf16[16,26,128]{2,1,0:T(8,128)(2,1)S(1)}, u32[]{:S(2)}, u32[]{:S(2)}) async-start(bf16[16,26,128]{2,1,0:T(8,128)(2,1)} %select_select_fusion.1), calls=%async_computation | async-start | bytes 262144 | tf_op jit(solution)/shard_map/all_to_all | solution.py:48
  396.9 0.1 fusion.25
  397.0 7.7 %all-to-all-done = bf16[16,26,128]{2,1,0:T(8,128)(2,1)S(1)} async-done(((bf16[16,26,128]{2,1,0:T(8,128)(2,1)}), bf16[16,26,128]{2,1,0:T(8,128)(2,1)S(1)}, u32[]{:S(2)}, u32[]{:S(2)}) %all-to-all-start) | async-done | bytes 106528 | tf_op jit(solution)/shard_map/all_to_all | solution.py:48
  404.8 2.4 gather_fusion.1
  407.2 1.0 select_select_fusion
  408.2 3.5 all-to-all-start.1
  411.7 0.6 fusion.26
  412.3 1.3 iota_compare_fusion.1
  413.6 6.4 %all-to-all-done.1 = bf16[16,52,128]{2,1,0:T(8,128)(2,1)S(1)} async-done(((bf16[16,52,128]{2,1,0:T(8,128)(2,1)}), bf16[16,52,128]{2,1,0:T(8,128)(2,1)S(1)}, u32[]{:S(2)}, u32[]{:S(2)}) %all-to-all-start.1) | async-done | bytes 213024 | tf_op jit(solution)/shard_map/all_to_all | solution.py:59
  420.1 2.4 gather_fusion.2
  422.4 1.0 fusion
  (13 shorter events, 0.2 us)
Async XLA Ops:
  0.6 77.0 %collective-permute-start = (f32[32,26624]{1,0:T(8,128)}, f32[32,26624]{1,0:T(8,128)S(1)}, u32[]{:S(2)}, u32[]{:S(2)}) collective-permute-start(f32[32,26624]{1,0:T(8,128)} %bitcast.8), channel_id=1, source_target_pairs={{0,2},{2,0},{4,6},{6,4},{8,10},{10,8},{12,14},{14,12},{16,18},{18,... | collective-permute-start | bytes 10223624 | tf_op jit(solution)/shard_map/ppermute | solution.py:20
  80.0 74.9 %collective-permute-start.1 = (f32[32,26624]{1,0:T(8,128)S(1)}, f32[32,26624]{1,0:T(8,128)S(1)}, u32[]{:S(2)}, u32[]{:S(2)}) collective-permute-start(f32[32,26624]{1,0:T(8,128)S(1)} %bitcast_add_fusion), channel_id=1, source_target_pairs={{0,4},{2,6},{4,0},{6,2},{8,12},{10,14},{12,8},{14,10},{16,20},{18,... | collective-permute-start | bytes 10223624 | tf_op jit(solution)/shard_map/ppermute | solution.py:20
  155.3 77.0 %copy-start = (s32[16]{0:T(128)S(1)}, s32[16]{0:T(128)}, u32[]{:S(2)}) copy-start(s32[16]{0:T(128)} %param.8) | copy-start | bytes 196
  155.3 77.2 %copy-start.1 = (s32[16]{0:T(128)S(1)}, s32[16]{0:T(128)}, u32[]{:S(2)}) copy-start(s32[16]{0:T(128)} %param.9) | copy-start | bytes 196
  155.3 74.1 %collective-permute-start.2 = (f32[32,26624]{1,0:T(8,128)S(1)}, f32[32,26624]{1,0:T(8,128)S(1)}, u32[]{:S(2)}, u32[]{:S(2)}) collective-permute-start(f32[32,26624]{1,0:T(8,128)S(1)} %add.291), channel_id=1, source_target_pairs={{0,8},{2,10},{4,12},{6,14},{8,0},{10,2},{12,4},{14,6},{16,24},{18,... | collective-permute-start | bytes 10223624 | tf_op jit(solution)/shard_map/ppermute | solution.py:20
  229.8 147.3 %collective-permute-start.3 = (f32[32,26624]{1,0:T(8,128)S(1)}, f32[32,26624]{1,0:T(8,128)}, u32[]{:S(2)}, u32[]{:S(2)}) collective-permute-start(f32[32,26624]{1,0:T(8,128)S(1)} %add.292), channel_id=1, source_target_pairs={{0,16},{2,18},{4,20},{6,22},{8,24},{10,26},{12,28},{14,30},{16,0},... | collective-permute-start | bytes 10223624 | tf_op jit(solution)/shard_map/ppermute | solution.py:20
  390.8 14.0 %all-to-all-start = ((bf16[16,26,128]{2,1,0:T(8,128)(2,1)}), bf16[16,26,128]{2,1,0:T(8,128)(2,1)S(1)}, u32[]{:S(2)}, u32[]{:S(2)}) async-start(bf16[16,26,128]{2,1,0:T(8,128)(2,1)} %select_select_fusion.1), calls=%async_computation | async-start | bytes 262144 | tf_op jit(solution)/shard_map/all_to_all | solution.py:48
  408.2 11.8 %all-to-all-start.1 = ((bf16[16,52,128]{2,1,0:T(8,128)(2,1)}), bf16[16,52,128]{2,1,0:T(8,128)(2,1)S(1)}, u32[]{:S(2)}, u32[]{:S(2)}) async-start(bf16[16,52,128]{2,1,0:T(8,128)(2,1)} %select_select_fusion), calls=%async_computation.1 | async-start | bytes 458752 | tf_op jit(solution)/shard_map/all_to_all | solution.py:59
